TPU v7x, 32 devices: a whole 2x2x4 slice. The times are simulated.
32 devices in a mesh: row: 4 (over z), col: 8 (over y, x, core).
Axes of the slice: x: 2, y: 2, z: 4, core: 2. Of those that a mesh axis runs over, the one named last changes fastest.
Arguments:
- points: float32 [16, 32768], P(None, ('row', 'col')), may hold values from -6 to 6
- inverse_scales: float32 [16], replicated, may hold values from 0.05 to 31.255105
- probe_signs: int32 [32768, 128], P(('row', 'col')), may hold values 0 or 1
Outputs:
- trace_terms: float32 [128], replicated
- logdet_terms: float32 [128], replicated
All inputs are finite; a program needn't handle non-finite values. No bound on the sum of `probe_signs` on one device may be relied on, other than what follows from the above.
Results may differ from a plain program's by a relative error of at most 0.0014.
Values may be sent and summed in bfloat16 or wider, within the bound.
A program may use at most 128 MiB of HBM per device.

v0:
```python
import math
import jax
import jax.numpy as jnp
from jax import lax
from jax.sharding import PartitionSpec as P

STEPS = 3
epsilon = 1e-06
noise_level = 1.0
jacobi_sweeps = 6


def kernel_block(left_points, right_points):
    cross_term = lax.dot_general(
        left_points,
        right_points,
        (((0,), (0,)), ((), ())),
        precision=lax.Precision.HIGHEST,
        preferred_element_type=jnp.float32,
    )
    left_norms = jnp.sum(left_points * left_points, axis=0)
    right_norms = jnp.sum(right_points * right_points, axis=0)
    distance = jnp.maximum(left_norms[:, None] + right_norms[None, :] - 2.0 * cross_term, 0.0)
    return jnp.exp(-0.5 * distance).astype(jnp.bfloat16)


def form_blocks(row_points, col_points):
    total_rows = row_points.shape[1]
    block_rows = math.gcd(total_rows, 512)
    blocked = row_points.reshape(
        row_points.shape[0], total_rows // block_rows, block_rows
    ).transpose(1, 0, 2)
    stacked = lax.map(lambda block_points: kernel_block(block_points, col_points), blocked)
    return stacked.reshape(total_rows, col_points.shape[1])


def log_weight(alpha_list, beta_list):
    degree = len(alpha_list)
    width_probes = alpha_list[0].shape[0]
    zeros_row = jnp.zeros((width_probes,), jnp.float32)
    ones_row = jnp.ones((width_probes,), jnp.float32)
    matrix = []
    vectors = []
    for first_idx in range(degree):
        entries = []
        basis_row = []
        for second_idx in range(degree):
            if first_idx == second_idx:
                entries.append(alpha_list[first_idx])
                basis_row.append(ones_row)
            elif abs(first_idx - second_idx) == 1:
                entries.append(beta_list[min(first_idx, second_idx)])
                basis_row.append(zeros_row)
            else:
                entries.append(zeros_row)
                basis_row.append(zeros_row)
        matrix.append(entries)
        vectors.append(basis_row)
    for sweep_index in range(jacobi_sweeps):
        for first_idx in range(degree):
            for second_idx in range(first_idx + 1, degree):
                coupling = matrix[first_idx][second_idx]
                rotate_by = 0.5 * jnp.arctan2(
                    2.0 * coupling, matrix[second_idx][second_idx] - matrix[first_idx][first_idx]
                )
                cosine = jnp.cos(rotate_by)
                sine_val = jnp.sin(rotate_by)
                for row_idx in range(degree):
                    left_val = matrix[row_idx][first_idx]
                    right_val = matrix[row_idx][second_idx]
                    matrix[row_idx][first_idx] = cosine * left_val - sine_val * right_val
                    matrix[row_idx][second_idx] = sine_val * left_val + cosine * right_val
                    left_vec = vectors[row_idx][first_idx]
                    right_vec = vectors[row_idx][second_idx]
                    vectors[row_idx][first_idx] = cosine * left_vec - sine_val * right_vec
                    vectors[row_idx][second_idx] = sine_val * left_vec + cosine * right_vec
                for col_idx in range(degree):
                    upper_val = matrix[first_idx][col_idx]
                    lower_val = matrix[second_idx][col_idx]
                    matrix[first_idx][col_idx] = cosine * upper_val - sine_val * lower_val
                    matrix[second_idx][col_idx] = sine_val * upper_val + cosine * lower_val
    total = zeros_row
    for index_k in range(degree):
        total = total + vectors[0][index_k] * vectors[0][index_k] * jnp.log(
            matrix[index_k][index_k]
        )
    return total


def per_device(points, inverse_scales, probe_signs):
    scaled = points * inverse_scales[:, None]
    row_points = lax.all_gather(scaled, "col", axis=1, tiled=True)
    col_points = lax.all_gather(scaled, "row", axis=1, tiled=True)
    cached = form_blocks(row_points, col_points)
    direction = 2.0 * probe_signs.astype(jnp.float32) - 1.0
    basis_prev = jnp.zeros_like(direction)
    alpha_list = []
    beta_list = []
    for lanczos_step in range(STEPS):
        squares = lax.psum(jnp.sum(direction * direction, axis=0), ("row", "col"))
        vector_half = direction.astype(jnp.bfloat16)
        gathered = lax.all_gather(vector_half, "col", axis=0, tiled=True)
        image = (
            lax.psum_scatter(
                lax.dot_general(
                    cached, gathered, (((0,), (0,)), ((), ())), preferred_element_type=jnp.float32
                ).astype(jnp.bfloat16),
                "row",
                scatter_dimension=0,
                tiled=True,
            ).astype(jnp.float32)
            + noise_level * direction
        )
        curvature = lax.psum(jnp.sum(direction * image, axis=0), ("row", "col"))
        beta_now = jnp.sqrt(squares + epsilon)
        alpha_now = curvature / (beta_now * beta_now)
        alpha_list.append(alpha_now)
        beta_list.append(beta_now)
        if lanczos_step + 1 < STEPS:
            basis_now = direction / beta_now
            direction = image / beta_now - alpha_now * basis_now - beta_now * basis_prev
            basis_prev = basis_now
    logdet_terms = log_weight(alpha_list, beta_list[1:])
    return (alpha_list[0], logdet_terms)


def solution(mesh):
    in_specs = (P(None, ("row", "col")), P(), P(("row", "col"), None))
    out_specs = (P(), P())
    return jax.shard_map(
        per_device, mesh=mesh, in_specs=in_specs, out_specs=out_specs, check_vma=False
    )
```

profile of v0, /device:TPU:0, one launch (start us, length us, event | category | flops | bytes accessed | tf_op | source)
XLA Modules:
  0.0 559.0 jit_solution(14007900071963346204)
XLA Ops:
  10.0 15.6 %all_gather.16 = f32[16,4096]{1,0:T(8,128)S(1)} all-gather(f32[16,1024]{1,0:T(8,128)S(1)} %broadcast_multiply_fusion), channel_id=1, replica_groups=mesh['row'=4,'col'=8] {'row'}, dimensions={1}, use_global_device_ids=true | all-gather | bytes 327680 | tf_op jit(solution)/shard_map/all_gather | solution.py:93
  25.7 11.0 %all_gather.15 = f32[16,8192]{1,0:T(8,128)S(1)} all-gather(f32[16,1024]{1,0:T(8,128)S(1)} %broadcast_multiply_fusion), channel_id=1, replica_groups=mesh['row'=4,'col'=8] {'col'}, dimensions={1}, use_global_device_ids=true | all-gather | bytes 589824 | tf_op jit(solution)/shard_map/all_gather | solution.py:92
  36.8 163.7 %while.12 = (s32[]{:T(128)}, bf16[16,512,4096]{2,1,0:T(8,128)(2,1)}, f32[16,16,512]{2,1,0:T(8,128)S(1)}, f32[4096]{0:T(1024)S(1)}, f32[16,4096]{1,0:T(8,128)S(1)}, /*index=5*/s32[]{:T(128)}) while((s32[]{:T(128)}, bf16[16,512,4096]{2,1,0:T(8,128)(2,1)}, f32[16,16,512]{2,1,0:T(8,128)S(1)}, f32[4096]{0:T(1024)S(1)}, f32[16,4096]{1,0:T(8,128)S(1)}, ...), condition=%wide.region_3.4_spmd, body=%wide.region_1.3_spmd.sunk | while | flops 415251968 | bytes 4543561 | solution.py:33
  36.8 10.2 %fusion.25 = bf16[16,512,4096]{2,1,0:T(8,128)(2,1)} fusion(bf16[16,512,4096]{2,1,0:T(8,128)(2,1)} %get-tuple-element.127, s32[]{:T(128)} %get-tuple-element.126, f32[16,4096]{1,0:T(8,128)S(1)} %get-tuple-element.136, f32[4096]{0:T(1024)S(1)} %get-tuple-element.135, f32[512]{0:T(512)S(1)} %fusion.24, f32[16,16,512]{2,1,0:T(8,128)S(1)} %get-tuple-element.134), kind=kOutput, calls=%fused_computation.2.clone.1 | convolution fusion | flops 415236096 | bytes 4508672 | tf_op jit(solution)/shard_map/while/body/eval_jaxpr/dot_general | solution.py:14
  57.3 10.2 %fusion.25 = bf16[16,512,4096]{2,1,0:T(8,128)(2,1)} fusion(bf16[16,512,4096]{2,1,0:T(8,128)(2,1)} %get-tuple-element.127, s32[]{:T(128)} %get-tuple-element.126, f32[16,4096]{1,0:T(8,128)S(1)} %get-tuple-element.136, f32[4096]{0:T(1024)S(1)} %get-tuple-element.135, f32[512]{0:T(512)S(1)} %fusion.24, f32[16,16,512]{2,1,0:T(8,128)S(1)} %get-tuple-element.134), kind=kOutput, calls=%fused_computation.2.clone.1 | convolution fusion | flops 415236096 | bytes 4508672 | tf_op jit(solution)/shard_map/while/body/eval_jaxpr/dot_general | solution.py:14
  77.8 10.2 %fusion.25 = bf16[16,512,4096]{2,1,0:T(8,128)(2,1)} fusion(bf16[16,512,4096]{2,1,0:T(8,128)(2,1)} %get-tuple-element.127, s32[]{:T(128)} %get-tuple-element.126, f32[16,4096]{1,0:T(8,128)S(1)} %get-tuple-element.136, f32[4096]{0:T(1024)S(1)} %get-tuple-element.135, f32[512]{0:T(512)S(1)} %fusion.24, f32[16,16,512]{2,1,0:T(8,128)S(1)} %get-tuple-element.134), kind=kOutput, calls=%fused_computation.2.clone.1 | convolution fusion | flops 415236096 | bytes 4508672 | tf_op jit(solution)/shard_map/while/body/eval_jaxpr/dot_general | solution.py:14
  98.2 10.2 %fusion.25 = bf16[16,512,4096]{2,1,0:T(8,128)(2,1)} fusion(bf16[16,512,4096]{2,1,0:T(8,128)(2,1)} %get-tuple-element.127, s32[]{:T(128)} %get-tuple-element.126, f32[16,4096]{1,0:T(8,128)S(1)} %get-tuple-element.136, f32[4096]{0:T(1024)S(1)} %get-tuple-element.135, f32[512]{0:T(512)S(1)} %fusion.24, f32[16,16,512]{2,1,0:T(8,128)S(1)} %get-tuple-element.134), kind=kOutput, calls=%fused_computation.2.clone.1 | convolution fusion | flops 415236096 | bytes 4508672 | tf_op jit(solution)/shard_map/while/body/eval_jaxpr/dot_general | solution.py:14
  118.6 10.3 %fusion.25 = bf16[16,512,4096]{2,1,0:T(8,128)(2,1)} fusion(bf16[16,512,4096]{2,1,0:T(8,128)(2,1)} %get-tuple-element.127, s32[]{:T(128)} %get-tuple-element.126, f32[16,4096]{1,0:T(8,128)S(1)} %get-tuple-element.136, f32[4096]{0:T(1024)S(1)} %get-tuple-element.135, f32[512]{0:T(512)S(1)} %fusion.24, f32[16,16,512]{2,1,0:T(8,128)S(1)} %get-tuple-element.134), kind=kOutput, calls=%fused_computation.2.clone.1 | convolution fusion | flops 415236096 | bytes 4508672 | tf_op jit(solution)/shard_map/while/body/eval_jaxpr/dot_general | solution.py:14
  128.9 10.2 %fusion.25 = bf16[16,512,4096]{2,1,0:T(8,128)(2,1)} fusion(bf16[16,512,4096]{2,1,0:T(8,128)(2,1)} %get-tuple-element.127, s32[]{:T(128)} %get-tuple-element.126, f32[16,4096]{1,0:T(8,128)S(1)} %get-tuple-element.136, f32[4096]{0:T(1024)S(1)} %get-tuple-element.135, f32[512]{0:T(512)S(1)} %fusion.24, f32[16,16,512]{2,1,0:T(8,128)S(1)} %get-tuple-element.134), kind=kOutput, calls=%fused_computation.2.clone.1 | convolution fusion | flops 415236096 | bytes 4508672 | tf_op jit(solution)/shard_map/while/body/eval_jaxpr/dot_general | solution.py:14
  149.4 10.2 %fusion.25 = bf16[16,512,4096]{2,1,0:T(8,128)(2,1)} fusion(bf16[16,512,4096]{2,1,0:T(8,128)(2,1)} %get-tuple-element.127, s32[]{:T(128)} %get-tuple-element.126, f32[16,4096]{1,0:T(8,128)S(1)} %get-tuple-element.136, f32[4096]{0:T(1024)S(1)} %get-tuple-element.135, f32[512]{0:T(512)S(1)} %fusion.24, f32[16,16,512]{2,1,0:T(8,128)S(1)} %get-tuple-element.134), kind=kOutput, calls=%fused_computation.2.clone.1 | convolution fusion | flops 415236096 | bytes 4508672 | tf_op jit(solution)/shard_map/while/body/eval_jaxpr/dot_general | solution.py:14
  159.6 10.3 %fusion.25 = bf16[16,512,4096]{2,1,0:T(8,128)(2,1)} fusion(bf16[16,512,4096]{2,1,0:T(8,128)(2,1)} %get-tuple-element.127, s32[]{:T(128)} %get-tuple-element.126, f32[16,4096]{1,0:T(8,128)S(1)} %get-tuple-element.136, f32[4096]{0:T(1024)S(1)} %get-tuple-element.135, f32[512]{0:T(512)S(1)} %fusion.24, f32[16,16,512]{2,1,0:T(8,128)S(1)} %get-tuple-element.134), kind=kOutput, calls=%fused_computation.2.clone.1 | convolution fusion | flops 415236096 | bytes 4508672 | tf_op jit(solution)/shard_map/while/body/eval_jaxpr/dot_general | solution.py:14
  169.9 10.2 %fusion.25 = bf16[16,512,4096]{2,1,0:T(8,128)(2,1)} fusion(bf16[16,512,4096]{2,1,0:T(8,128)(2,1)} %get-tuple-element.127, s32[]{:T(128)} %get-tuple-element.126, f32[16,4096]{1,0:T(8,128)S(1)} %get-tuple-element.136, f32[4096]{0:T(1024)S(1)} %get-tuple-element.135, f32[512]{0:T(512)S(1)} %fusion.24, f32[16,16,512]{2,1,0:T(8,128)S(1)} %get-tuple-element.134), kind=kOutput, calls=%fused_computation.2.clone.1 | convolution fusion | flops 415236096 | bytes 4508672 | tf_op jit(solution)/shard_map/while/body/eval_jaxpr/dot_general | solution.py:14
  180.1 10.2 %fusion.25 = bf16[16,512,4096]{2,1,0:T(8,128)(2,1)} fusion(bf16[16,512,4096]{2,1,0:T(8,128)(2,1)} %get-tuple-element.127, s32[]{:T(128)} %get-tuple-element.126, f32[16,4096]{1,0:T(8,128)S(1)} %get-tuple-element.136, f32[4096]{0:T(1024)S(1)} %get-tuple-element.135, f32[512]{0:T(512)S(1)} %fusion.24, f32[16,16,512]{2,1,0:T(8,128)S(1)} %get-tuple-element.134), kind=kOutput, calls=%fused_computation.2.clone.1 | convolution fusion | flops 415236096 | bytes 4508672 | tf_op jit(solution)/shard_map/while/body/eval_jaxpr/dot_general | solution.py:14
  200.5 29.2 %convolution_convert_fusion.2 = bf16[4096,128]{1,0:T(8,128)(2,1)} fusion(bf16[8192,4096]{1,0:T(8,128)(2,1)} %bitcast.3, bf16[8192,128]{1,0:T(8,128)(2,1)} %all-gather.4.cloned.1.call-done), kind=kOutput, calls=%fused_computation.10 | convolution fusion | flops 8590458880 | bytes 70254592 | tf_op jit(solution)/shard_map/dot_general | solution.py:105
  229.7 28.3 %reduce-scatter.4.cloned.1.call-done = bf16[1024,128]{1,0:T(8,128)(2,1)} async-done(((bf16[4096,128]{1,0:T(8,128)(2,1)}), bf16[1024,128]{1,0:T(8,128)(2,1)}) %reduce-scatter.4.cloned.1.call-update) | async-done | bytes 262160 | tf_op jit(solution)/shard_map/reduce_scatter | solution.py:104
  259.2 38.9 %all-reduce.2 = (f32[128]{0:T(128)S(1)}, f32[128]{0:T(128)S(1)}) all-reduce(f32[128]{0:T(128)S(1)} %get-tuple-element.63, f32[128]{0:T(128)S(1)} %get-tuple-element.62), channel_id=1, replica_groups=mesh['row'=4,'col'=8] {'row','col'}, use_global_device_ids=true, to_apply=%region_6.7 | all-reduce | flops 256 | bytes 2048 | tf_op jit(solution)/shard_map/psum | solution.py:114
  300.0 27.6 %all-gather.6.cloned.1.call-done = bf16[8192,128]{1,0:T(8,128)(2,1)} async-done(((bf16[1024,128]{1,0:T(8,128)(2,1)}), bf16[8192,128]{1,0:T(8,128)(2,1)}) %all-gather.6.cloned.1.call-update) | async-done | bytes 2097168 | tf_op jit(solution)/shard_map/all_gather | solution.py:102
  327.6 29.1 %convolution_convert_fusion.1 = bf16[4096,128]{1,0:T(8,128)(2,1)} fusion(bf16[8192,4096]{1,0:T(8,128)(2,1)} %bitcast.3, bf16[8192,128]{1,0:T(8,128)(2,1)} %all-gather.6.cloned.1.call-done), kind=kOutput, calls=%fused_computation.9 | convolution fusion | flops 8590458880 | bytes 70254592 | tf_op jit(solution)/shard_map/dot_general | solution.py:105
  356.8 27.4 %reduce-scatter.6.cloned.1.call-done = bf16[1024,128]{1,0:T(8,128)(2,1)} async-done(((bf16[4096,128]{1,0:T(8,128)(2,1)}), bf16[1024,128]{1,0:T(8,128)(2,1)}) %reduce-scatter.6.cloned.1.call-update) | async-done | bytes 262160 | tf_op jit(solution)/shard_map/reduce_scatter | solution.py:104
  385.3 38.7 %all-reduce.1 = (f32[128]{0:T(128)S(1)}, f32[128]{0:T(128)S(1)}) all-reduce(f32[128]{0:T(128)S(1)} %get-tuple-element.61, f32[128]{0:T(128)S(1)} %get-tuple-element.60), channel_id=1, replica_groups=mesh['row'=4,'col'=8] {'row','col'}, use_global_device_ids=true, to_apply=%region_13.14 | all-reduce | flops 256 | bytes 2048 | tf_op jit(solution)/shard_map/psum | solution.py:114
  426.3 27.4 %all-gather.8.cloned.1.call-done = bf16[8192,128]{1,0:T(8,128)(2,1)} async-done(((bf16[1024,128]{1,0:T(8,128)(2,1)}), bf16[8192,128]{1,0:T(8,128)(2,1)}) %all-gather.8.cloned.1.call-update) | async-done | bytes 2097168 | tf_op jit(solution)/shard_map/all_gather | solution.py:102
  453.7 29.1 %convolution_convert_fusion = bf16[4096,128]{1,0:T(8,128)(2,1)} fusion(bf16[8192,4096]{1,0:T(8,128)(2,1)} %bitcast.3, bf16[8192,128]{1,0:T(8,128)(2,1)} %all-gather.8.cloned.1.call-done), kind=kOutput, calls=%fused_computation.8 | convolution fusion | flops 8590458880 | bytes 70254592 | tf_op jit(solution)/shard_map/dot_general | solution.py:105
  482.8 27.4 %reduce-scatter.8.cloned.1.call-done = bf16[1024,128]{1,0:T(8,128)(2,1)} async-done(((bf16[4096,128]{1,0:T(8,128)(2,1)}), bf16[1024,128]{1,0:T(8,128)(2,1)}) %reduce-scatter.8.cloned.1.call-update) | async-done | bytes 262160 | tf_op jit(solution)/shard_map/reduce_scatter | solution.py:104
  511.4 38.7 %all-reduce = (f32[128]{0:T(128)S(1)}, f32[128]{0:T(128)S(1)}) all-reduce(f32[128]{0:T(128)S(1)} %get-tuple-element.59, f32[128]{0:T(128)S(1)} %get-tuple-element.58), channel_id=1, replica_groups=mesh['row'=4,'col'=8] {'row','col'}, use_global_device_ids=true, to_apply=%region_18.19 | all-reduce | flops 256 | bytes 2048 | tf_op jit(solution)/shard_map/psum | solution.py:114
  (52 shorter events, 74.0 us)
Async XLA Ops:
  7.2 193.3 %all-gather.4.cloned.1.call-start = ((), (), s32[]{:S(2)}) async-start(), calls=%async_computation.3 | async-start | bytes 2359296 | tf_op jit(solution)/shard_map/all_gather | solution.py:102
  9.1 249.0 %reduce-scatter.4.cloned.1.call-start = ((), (), s32[]{:S(2)}) async-start(), calls=%async_computation.4 | async-start | bytes 1310720 | tf_op jit(solution)/shard_map/reduce_scatter | solution.py:104
  200.5 57.5 %copy-start = (s32[1024,128]{1,0:T(8,128)S(1)}, s32[1024,128]{1,0:T(8,128)}, u32[]{:S(2)}) copy-start(s32[1024,128]{1,0:T(8,128)} %param.7) | copy-start | bytes 1572868
  229.7 98.0 %all-gather.6.cloned.1.call-start = ((), (), s32[]{:S(2)}) async-start(), calls=%async_computation.5 | async-start | bytes 2359296 | tf_op jit(solution)/shard_map/all_gather | solution.py:102
  298.1 252.0 %copy-start.1 = (f32[128]{0:T(128)}, f32[128]{0:T(128)S(1)}, u32[]{:S(2)}) copy-start(f32[128]{0:T(128)S(1)} %get-tuple-element.87) | copy-start | bytes 1540
  300.0 84.3 %reduce-scatter.6.cloned.1.call-start = ((), (), s32[]{:S(2)}) async-start(), calls=%async_computation.6 | async-start | bytes 1310720 | tf_op jit(solution)/shard_map/reduce_scatter | solution.py:104
  356.8 96.9 %all-gather.8.cloned.1.call-start = ((), (), s32[]{:S(2)}) async-start(), calls=%async_computation.7 | async-start | bytes 2359296 | tf_op jit(solution)/shard_map/all_gather | solution.py:102
  426.0 84.3 %reduce-scatter.8.cloned.1.call-start = ((), (), s32[]{:S(2)}) async-start(), calls=%async_computation.8 | async-start | bytes 1310720 | tf_op jit(solution)/shard_map/reduce_scatter | solution.py:104
Sparse Core Ops, SparseCore 0:
  9.9 31.1 all-gather.3
  229.8 28.1 reduce-scatter.3
  300.1 27.5 all-gather.5
  356.9 27.2 reduce-scatter.5
  426.1 27.5 all-gather.7
  482.9 27.2 reduce-scatter.7
where the time goes:
time: 560 us; the launch traced here: 559 us
  matrix products  251 us (45%)
  blocking collectives  143 us (26%)
  waiting for transfers between devices  138 us (25%)
  between operations  14.1 us (3%)
  other arithmetic  12.3 us (2%)
    dot_general x16, matrix products, kernel_block(): lax.dot_general(left_points, right_points, (((0,), (0,)), ((), ())), prec...  163 us
    psum x3, blocking collectives, per_device(): curvature = lax.psum(jnp.sum(direction * image, axis=0), ('row', 'col'))  116 us
    dot_general x3, matrix products, per_device(): lax.dot_general(cached, gathered, (((0,), (0,)), ((), ())), preferred_ele...  87.4 us
    reduce_scatter x3, waiting for transfers between devices, per_device(): lax.psum_scatter(lax.dot_general(cached, gathered, (((0,), (0,)), ((), ()...  83.2 us
    all_gather x3, waiting for transfers between devices, per_device(): gathered = lax.all_gather(vector_half, 'col', axis=0, tiled=True)  55.1 us
    all_gather x1, blocking collectives, per_device(): col_points = lax.all_gather(scaled, 'row', axis=1, tiled=True)  15.6 us
  transfers between devices with their start and end apart: 6, of which 5 were waited for; matrix products, arithmetic and copies ran while one was open for 29% of the time, Pallas kernels for 0%

commit v1 on v0

--- a/solution.py
+++ b/solution.py
@@ -111,7 +111,7 @@
             ).astype(jnp.float32)
             + noise_level * direction
         )
-        curvature = lax.psum(jnp.sum(direction * image, axis=0), ("row", "col"))
+        curvature = lax.psum(lax.psum(jnp.sum(direction * image, axis=0), "col"), "row")
         beta_now = jnp.sqrt(squares + epsilon)
         alpha_now = curvature / (beta_now * beta_now)
         alpha_list.append(alpha_now)

time: 560 us -> 626 us (1.12)
  blocking collectives: 143 us -> 210 us
    psum x3 -> x9, blocking collectives: 116 us -> 184 us  [the longest x3 116 us: per_device(): squares = lax.psum(jnp.sum(direction * direction, axis=0), ('row', 'col'))]
  transfers between devices with their start and end apart: 6 -> 6, of which waited for: 5 -> 5; matrix products, arithmetic and copies ran while one was open for 29% -> 26% of each run, Pallas kernels for 0% -> 0%
where the time goes in v1:
time: 626 us; the launch traced here: 625 us
  matrix products  251 us (40%)
  blocking collectives  210 us (34%)
  waiting for transfers between devices  137 us (22%)
  between operations  14.1 us (2%)
  other arithmetic  12.3 us (2%)
    dot_general x16, matrix products, kernel_block(): lax.dot_general(left_points, right_points, (((0,), (0,)), ((), ())), prec...  163 us
    psum x3, blocking collectives, per_device(): squares = lax.psum(jnp.sum(direction * direction, axis=0), ('row', 'col'))  116 us
    dot_general x3, matrix products, per_device(): lax.dot_general(cached, gathered, (((0,), (0,)), ((), ())), preferred_ele...  87.4 us
    reduce_scatter x3, waiting for transfers between devices, per_device(): lax.psum_scatter(lax.dot_general(cached, gathered, (((0,), (0,)), ((), ()...  83.2 us
    all_gather x3, waiting for transfers between devices, per_device(): gathered = lax.all_gather(vector_half, 'col', axis=0, tiled=True)  53.6 us
    psum x3, blocking collectives, per_device(): lax.psum(jnp.sum(direction * image, axis=0), 'col')  39.6 us
    psum x3, blocking collectives, per_device(): lax.psum(lax.psum(jnp.sum(direction * image, axis=0), 'col'), 'row')  27.6 us
    all_gather x1, blocking collectives, per_device(): col_points = lax.all_gather(scaled, 'row', axis=1, tiled=True)  15.6 us
  transfers between devices with their start and end apart: 6, of which 5 were waited for; matrix products, arithmetic and copies ran while one was open for 26% of the time, Pallas kernels for 0%

profile of v1, /device:TPU:0, one launch (start us, length us, event | category | flops | bytes accessed | tf_op | source)
XLA Modules:
  0.0 624.9 jit_solution(13648169769022380451)
XLA Ops:
  10.0 15.6 %all_gather.16 = f32[16,4096]{1,0:T(8,128)S(1)} all-gather(f32[16,1024]{1,0:T(8,128)S(1)} %broadcast_multiply_fusion), channel_id=1, replica_groups=mesh['row'=4,'col'=8] {'row'}, dimensions={1}, use_global_device_ids=true | all-gather | bytes 327680 | tf_op jit(solution)/shard_map/all_gather | solution.py:93
  25.7 11.0 %all_gather.15 = f32[16,8192]{1,0:T(8,128)S(1)} all-gather(f32[16,1024]{1,0:T(8,128)S(1)} %broadcast_multiply_fusion), channel_id=1, replica_groups=mesh['row'=4,'col'=8] {'col'}, dimensions={1}, use_global_device_ids=true | all-gather | bytes 589824 | tf_op jit(solution)/shard_map/all_gather | solution.py:92
  36.8 163.7 %while.12 = (s32[]{:T(128)}, bf16[16,512,4096]{2,1,0:T(8,128)(2,1)}, f32[16,16,512]{2,1,0:T(8,128)S(1)}, f32[4096]{0:T(1024)S(1)}, f32[16,4096]{1,0:T(8,128)S(1)}, /*index=5*/s32[]{:T(128)}) while((s32[]{:T(128)}, bf16[16,512,4096]{2,1,0:T(8,128)(2,1)}, f32[16,16,512]{2,1,0:T(8,128)S(1)}, f32[4096]{0:T(1024)S(1)}, f32[16,4096]{1,0:T(8,128)S(1)}, ...), condition=%wide.region_3.4_spmd, body=%wide.region_1.3_spmd.sunk | while | flops 415251968 | bytes 4543561 | solution.py:33
  36.8 10.2 %fusion.25 = bf16[16,512,4096]{2,1,0:T(8,128)(2,1)} fusion(bf16[16,512,4096]{2,1,0:T(8,128)(2,1)} %get-tuple-element.121, s32[]{:T(128)} %get-tuple-element.120, f32[16,4096]{1,0:T(8,128)S(1)} %get-tuple-element.130, f32[4096]{0:T(1024)S(1)} %get-tuple-element.129, f32[512]{0:T(512)S(1)} %fusion.24, f32[16,16,512]{2,1,0:T(8,128)S(1)} %get-tuple-element.128), kind=kOutput, calls=%fused_computation.2.clone.1 | convolution fusion | flops 415236096 | bytes 4508672 | tf_op jit(solution)/shard_map/while/body/eval_jaxpr/dot_general | solution.py:14
  57.3 10.2 %fusion.25 = bf16[16,512,4096]{2,1,0:T(8,128)(2,1)} fusion(bf16[16,512,4096]{2,1,0:T(8,128)(2,1)} %get-tuple-element.121, s32[]{:T(128)} %get-tuple-element.120, f32[16,4096]{1,0:T(8,128)S(1)} %get-tuple-element.130, f32[4096]{0:T(1024)S(1)} %get-tuple-element.129, f32[512]{0:T(512)S(1)} %fusion.24, f32[16,16,512]{2,1,0:T(8,128)S(1)} %get-tuple-element.128), kind=kOutput, calls=%fused_computation.2.clone.1 | convolution fusion | flops 415236096 | bytes 4508672 | tf_op jit(solution)/shard_map/while/body/eval_jaxpr/dot_general | solution.py:14
  77.8 10.2 %fusion.25 = bf16[16,512,4096]{2,1,0:T(8,128)(2,1)} fusion(bf16[16,512,4096]{2,1,0:T(8,128)(2,1)} %get-tuple-element.121, s32[]{:T(128)} %get-tuple-element.120, f32[16,4096]{1,0:T(8,128)S(1)} %get-tuple-element.130, f32[4096]{0:T(1024)S(1)} %get-tuple-element.129, f32[512]{0:T(512)S(1)} %fusion.24, f32[16,16,512]{2,1,0:T(8,128)S(1)} %get-tuple-element.128), kind=kOutput, calls=%fused_computation.2.clone.1 | convolution fusion | flops 415236096 | bytes 4508672 | tf_op jit(solution)/shard_map/while/body/eval_jaxpr/dot_general | solution.py:14
  98.2 10.2 %fusion.25 = bf16[16,512,4096]{2,1,0:T(8,128)(2,1)} fusion(bf16[16,512,4096]{2,1,0:T(8,128)(2,1)} %get-tuple-element.121, s32[]{:T(128)} %get-tuple-element.120, f32[16,4096]{1,0:T(8,128)S(1)} %get-tuple-element.130, f32[4096]{0:T(1024)S(1)} %get-tuple-element.129, f32[512]{0:T(512)S(1)} %fusion.24, f32[16,16,512]{2,1,0:T(8,128)S(1)} %get-tuple-element.128), kind=kOutput, calls=%fused_computation.2.clone.1 | convolution fusion | flops 415236096 | bytes 4508672 | tf_op jit(solution)/shard_map/while/body/eval_jaxpr/dot_general | solution.py:14
  118.6 10.3 %fusion.25 = bf16[16,512,4096]{2,1,0:T(8,128)(2,1)} fusion(bf16[16,512,4096]{2,1,0:T(8,128)(2,1)} %get-tuple-element.121, s32[]{:T(128)} %get-tuple-element.120, f32[16,4096]{1,0:T(8,128)S(1)} %get-tuple-element.130, f32[4096]{0:T(1024)S(1)} %get-tuple-element.129, f32[512]{0:T(512)S(1)} %fusion.24, f32[16,16,512]{2,1,0:T(8,128)S(1)} %get-tuple-element.128), kind=kOutput, calls=%fused_computation.2.clone.1 | convolution fusion | flops 415236096 | bytes 4508672 | tf_op jit(solution)/shard_map/while/body/eval_jaxpr/dot_general | solution.py:14
  159.6 10.3 %fusion.25 = bf16[16,512,4096]{2,1,0:T(8,128)(2,1)} fusion(bf16[16,512,4096]{2,1,0:T(8,128)(2,1)} %get-tuple-element.121, s32[]{:T(128)} %get-tuple-element.120, f32[16,4096]{1,0:T(8,128)S(1)} %get-tuple-element.130, f32[4096]{0:T(1024)S(1)} %get-tuple-element.129, f32[512]{0:T(512)S(1)} %fusion.24, f32[16,16,512]{2,1,0:T(8,128)S(1)} %get-tuple-element.128), kind=kOutput, calls=%fused_computation.2.clone.1 | convolution fusion | flops 415236096 | bytes 4508672 | tf_op jit(solution)/shard_map/while/body/eval_jaxpr/dot_general | solution.py:14
  169.9 10.2 %fusion.25 = bf16[16,512,4096]{2,1,0:T(8,128)(2,1)} fusion(bf16[16,512,4096]{2,1,0:T(8,128)(2,1)} %get-tuple-element.121, s32[]{:T(128)} %get-tuple-element.120, f32[16,4096]{1,0:T(8,128)S(1)} %get-tuple-element.130, f32[4096]{0:T(1024)S(1)} %get-tuple-element.129, f32[512]{0:T(512)S(1)} %fusion.24, f32[16,16,512]{2,1,0:T(8,128)S(1)} %get-tuple-element.128), kind=kOutput, calls=%fused_computation.2.clone.1 | convolution fusion | flops 415236096 | bytes 4508672 | tf_op jit(solution)/shard_map/while/body/eval_jaxpr/dot_general | solution.py:14
  200.5 29.2 %convolution_convert_fusion.2 = bf16[4096,128]{1,0:T(8,128)(2,1)} fusion(bf16[8192,4096]{1,0:T(8,128)(2,1)} %bitcast.3, bf16[8192,128]{1,0:T(8,128)(2,1)} %all-gather.4.cloned.1.call-done), kind=kOutput, calls=%fused_computation.10 | convolution fusion | flops 8590458880 | bytes 70254592 | tf_op jit(solution)/shard_map/dot_general | solution.py:105
  229.7 28.3 %reduce-scatter.4.cloned.1.call-done = bf16[1024,128]{1,0:T(8,128)(2,1)} async-done(((bf16[4096,128]{1,0:T(8,128)(2,1)}), bf16[1024,128]{1,0:T(8,128)(2,1)}) %reduce-scatter.4.cloned.1.call-update) | async-done | bytes 262160 | tf_op jit(solution)/shard_map/reduce_scatter | solution.py:104
  259.2 13.2 %psum.63 = f32[128]{0:T(128)S(1)} all-reduce(f32[128]{0:T(128)S(1)} %get-tuple-element.63), channel_id=1, replica_groups=mesh['row'=4,'col'=8] {'col'}, use_global_device_ids=true, to_apply=%region_6.7 | all-reduce | flops 128 | bytes 1024 | tf_op jit(solution)/shard_map/psum | solution.py:114
  281.7 38.8 %psum.65 = f32[128]{0:T(128)S(1)} all-reduce(f32[128]{0:T(128)S(1)} %get-tuple-element.62), channel_id=1, replica_groups=mesh['row'=4,'col'=8] {'row','col'}, use_global_device_ids=true, to_apply=%region_9.10 | all-reduce | flops 128 | bytes 1024 | tf_op jit(solution)/shard_map/psum | solution.py:100
  322.5 26.9 %all-gather.6.cloned.1.call-done = bf16[8192,128]{1,0:T(8,128)(2,1)} async-done(((bf16[1024,128]{1,0:T(8,128)(2,1)}), bf16[8192,128]{1,0:T(8,128)(2,1)}) %all-gather.6.cloned.1.call-update) | async-done | bytes 2097168 | tf_op jit(solution)/shard_map/all_gather | solution.py:102
  349.4 29.1 %convolution_convert_fusion.1 = bf16[4096,128]{1,0:T(8,128)(2,1)} fusion(bf16[8192,4096]{1,0:T(8,128)(2,1)} %bitcast.3, bf16[8192,128]{1,0:T(8,128)(2,1)} %all-gather.6.cloned.1.call-done), kind=kOutput, calls=%fused_computation.9 | convolution fusion | flops 8590458880 | bytes 70254592 | tf_op jit(solution)/shard_map/dot_general | solution.py:105
  378.6 27.4 %reduce-scatter.6.cloned.1.call-done = bf16[1024,128]{1,0:T(8,128)(2,1)} async-done(((bf16[4096,128]{1,0:T(8,128)(2,1)}), bf16[1024,128]{1,0:T(8,128)(2,1)}) %reduce-scatter.6.cloned.1.call-update) | async-done | bytes 262160 | tf_op jit(solution)/shard_map/reduce_scatter | solution.py:104
  407.1 13.2 %psum.67 = f32[128]{0:T(128)S(1)} all-reduce(f32[128]{0:T(128)S(1)} %get-tuple-element.61), channel_id=1, replica_groups=mesh['row'=4,'col'=8] {'col'}, use_global_device_ids=true, to_apply=%region_14.15 | all-reduce | flops 128 | bytes 1024 | tf_op jit(solution)/shard_map/psum | solution.py:114
  429.4 38.8 %psum.66 = f32[128]{0:T(128)S(1)} all-reduce(f32[128]{0:T(128)S(1)} %get-tuple-element.60), channel_id=1, replica_groups=mesh['row'=4,'col'=8] {'row','col'}, use_global_device_ids=true, to_apply=%region_11.12 | all-reduce | flops 128 | bytes 1024 | tf_op jit(solution)/shard_map/psum | solution.py:100
  470.5 26.7 %all-gather.8.cloned.1.call-done = bf16[8192,128]{1,0:T(8,128)(2,1)} async-done(((bf16[1024,128]{1,0:T(8,128)(2,1)}), bf16[8192,128]{1,0:T(8,128)(2,1)}) %all-gather.8.cloned.1.call-update) | async-done | bytes 2097168 | tf_op jit(solution)/shard_map/all_gather | solution.py:102
  497.2 29.1 %convolution_convert_fusion = bf16[4096,128]{1,0:T(8,128)(2,1)} fusion(bf16[8192,4096]{1,0:T(8,128)(2,1)} %bitcast.3, bf16[8192,128]{1,0:T(8,128)(2,1)} %all-gather.8.cloned.1.call-done), kind=kOutput, calls=%fused_computation.8 | convolution fusion | flops 8590458880 | bytes 70254592 | tf_op jit(solution)/shard_map/dot_general | solution.py:105
  526.3 27.4 %reduce-scatter.8.cloned.1.call-done = bf16[1024,128]{1,0:T(8,128)(2,1)} async-done(((bf16[4096,128]{1,0:T(8,128)(2,1)}), bf16[1024,128]{1,0:T(8,128)(2,1)}) %reduce-scatter.8.cloned.1.call-update) | async-done | bytes 262160 | tf_op jit(solution)/shard_map/reduce_scatter | solution.py:104
  554.9 13.2 %psum.70 = f32[128]{0:T(128)S(1)} all-reduce(f32[128]{0:T(128)S(1)} %get-tuple-element.59), channel_id=1, replica_groups=mesh['row'=4,'col'=8] {'col'}, use_global_device_ids=true, to_apply=%region_20.21 | all-reduce | flops 128 | bytes 1024 | tf_op jit(solution)/shard_map/psum | solution.py:114
  577.2 38.8 %psum.69 = f32[128]{0:T(128)S(1)} all-reduce(f32[128]{0:T(128)S(1)} %get-tuple-element.58), channel_id=1, replica_groups=mesh['row'=4,'col'=8] {'row','col'}, use_global_device_ids=true, to_apply=%region_17.18 | all-reduce | flops 128 | bytes 1024 | tf_op jit(solution)/shard_map/psum | solution.py:100
  (58 shorter events, 132.3 us)
Async XLA Ops:
  7.2 193.3 %all-gather.4.cloned.1.call-start = ((), (), s32[]{:S(2)}) async-start(), calls=%async_computation.3 | async-start | bytes 2359296 | tf_op jit(solution)/shard_map/all_gather | solution.py:102
  9.1 249.0 %reduce-scatter.4.cloned.1.call-start = ((), (), s32[]{:S(2)}) async-start(), calls=%async_computation.4 | async-start | bytes 1310720 | tf_op jit(solution)/shard_map/reduce_scatter | solution.py:104
  200.5 57.5 %copy-start = (s32[1024,128]{1,0:T(8,128)S(1)}, s32[1024,128]{1,0:T(8,128)}, u32[]{:S(2)}) copy-start(s32[1024,128]{1,0:T(8,128)} %param.7) | copy-start | bytes 1572868
  229.7 119.7 %all-gather.6.cloned.1.call-start = ((), (), s32[]{:S(2)}) async-start(), calls=%async_computation.5 | async-start | bytes 2359296 | tf_op jit(solution)/shard_map/all_gather | solution.py:102
  320.5 295.5 %copy-start.1 = (f32[128]{0:T(128)}, f32[128]{0:T(128)S(1)}, u32[]{:S(2)}) copy-start(f32[128]{0:T(128)S(1)} %get-tuple-element.81) | copy-start | bytes 1540
  322.4 83.5 %reduce-scatter.6.cloned.1.call-start = ((), (), s32[]{:S(2)}) async-start(), calls=%async_computation.6 | async-start | bytes 1310720 | tf_op jit(solution)/shard_map/reduce_scatter | solution.py:104
  378.5 118.6 %all-gather.8.cloned.1.call-start = ((), (), s32[]{:S(2)}) async-start(), calls=%async_computation.7 | async-start | bytes 2359296 | tf_op jit(solution)/shard_map/all_gather | solution.py:102
  470.2 83.6 %reduce-scatter.8.cloned.1.call-start = ((), (), s32[]{:S(2)}) async-start(), calls=%async_computation.8 | async-start | bytes 1310720 | tf_op jit(solution)/shard_map/reduce_scatter | solution.py:104
Sparse Core Ops, SparseCore 0:
  9.9 31.1 all-gather.3
  229.8 28.1 reduce-scatter.3
  322.6 26.7 all-gather.5
  378.7 27.2 reduce-scatter.5
  470.3 26.8 all-gather.7
  526.4 27.2 reduce-scatter.7
